TPU v7x, 256 devices: a whole 4x4x8 slice. The times are simulated.
256 devices in a mesh: branch: 2 (over z_lo), batch: 32 (over y, z_hi, core), rows: 4 (over x).
Axes of the slice: x: 4, y: 4, z: 8 (z_hi: 4, z_lo: 2; z = z_hi * 2 + z_lo), core: 2. Of those that a mesh axis runs over, the one named last changes fastest.
Arguments:
- timestep: int32 [32], P('batch'), parts along dimension 0, may hold values from 0 to 999
- features: bfloat16 [32, 2, 32, 64, 640], P('batch', 'branch', 'rows'), parts along dimension 0, may hold values from -6 to 6
- conv1_weight: bfloat16 [2, 3, 3, 640, 640], P('branch', None, None, None, 'rows'), may hold values from -0.078125 to 0.078125
- conv1_bias: float32 [2, 640], P('branch'), may hold values from -3 to 3
- conv2_weight: bfloat16 [2, 3, 3, 640, 640], P('branch', None, None, None, 'rows'), may hold values from -0.078125 to 0.078125
- conv2_bias: float32 [2, 640], P('branch'), may hold values from -3 to 3
- norm1_gain: float32 [2, 640], P('branch'), may hold values from 0.25 to 1.75
- norm1_shift: float32 [2, 640], P('branch'), may hold values from -3 to 3
- norm2_gain: float32 [2, 640], P('branch'), may hold values from 0.25 to 1.75
- norm2_shift: float32 [2, 640], P('branch'), may hold values from -3 to 3
- time_weight: bfloat16 [2, 320, 1280], P('branch'), may hold values from -0.3125 to 0.3125
- emb_weight: bfloat16 [2, 1280, 640], P('branch'), may hold values from -0.15625 to 0.15625
- zero_weight: bfloat16 [640, 640], replicated, may hold values from -0.25 to 0.25
- zero_bias: float32 [640], replicated, may hold values from -3 to 3
Outputs:
- block_out: bfloat16 [32, 2, 32, 64, 640], P('batch', 'branch', 'rows'), parts along dimension 0
There are 32 independent parts, one for each index of `batch`. A program takes and returns all parts, laid end to end along the dimension named above; an argument that names none is the same for every part. Nothing has to cross between parts.
All inputs are finite; a program needn't handle non-finite values.
Results may differ from a plain program's by a relative error of at most 0.01.
Values may be sent and summed in bfloat16 or wider, within the bound.
A program may use at most 128 MiB of HBM per device.

v0:
```python
import math
import jax
import jax.numpy as jnp
from jax import lax
from jax.sharding import PartitionSpec as P

GROUPS = 32


def from_everyone(x, axis):
    copies = jnp.broadcast_to(x, (lax.axis_size(axis), *x.shape))
    return lax.all_to_all(copies, axis, split_axis=0, concat_axis=0, tiled=True)


def laid_out(pieces, dim):
    pieces = jnp.moveaxis(pieces, 0, dim)
    dims = pieces.shape
    return pieces.reshape(*dims[:dim], dims[dim] * dims[dim + 1], *dims[dim + 2 :])


def gathered_copies(x, axis, dim):
    pieces = from_everyone(x, axis)
    return laid_out(pieces, dim)


def as_sent(x):

    def short(part):
        return part.astype(jnp.bfloat16) if part.dtype == jnp.float32 else part

    return jax.tree.map(short, x)


def from_behind(x, axis, by):
    length = lax.axis_size(axis)
    pairs = [(i, i + by) for i in range(length) if 0 <= i + by < length]
    return lax.ppermute(x, axis, pairs)


def sinusoid(timestep, count):
    half = count // 2
    freqs = jnp.exp(-math.log(10000.0) * jnp.arange(half, dtype=jnp.float32) / half)
    angles = timestep.astype(jnp.float32)[0] * freqs
    return jnp.concatenate([jnp.cos(angles), jnp.sin(angles)])


def time_shift(timestep, time_weight, emb_weight):
    waves = sinusoid(timestep, time_weight.shape[0])
    inner = jax.nn.silu(jnp.dot(waves, time_weight.astype(jnp.float32)))
    return jnp.dot(inner, emb_weight.astype(jnp.float32))


def group_sums(values, groups):
    rows, cols, chans = values.shape
    grouped = values.reshape(rows, cols, groups, chans // groups)
    return (jnp.sum(grouped, axis=(0, 1, 3)), jnp.sum(grouped * grouped, axis=(0, 1, 3)))


def apply_norm(values, total, square, count, gain, shift):
    rows, cols, chans = values.shape
    groups = total.shape[0]
    mean = total / count
    var = square / count - mean * mean
    grouped = values.reshape(rows, cols, groups, chans // groups)
    normed = (grouped - mean[:, None]) * lax.rsqrt(var + 1e-05)[:, None]
    return jax.nn.silu(normed.reshape(values.shape) * gain + shift).astype(jnp.bfloat16)


def convolve(inputs, kernel, padding):
    return lax.conv_general_dilated(
        inputs[None],
        kernel,
        (1, 1),
        padding,
        dimension_numbers=("NHWC", "HWIO", "NHWC"),
        preferred_element_type=jnp.float32,
    )[0]


def body(
    timestep,
    features,
    conv1_weight,
    conv1_bias,
    conv2_weight,
    conv2_bias,
    norm1_gain,
    norm1_shift,
    norm2_gain,
    norm2_shift,
    time_weight,
    emb_weight,
    zero_weight,
    zero_bias,
):
    inputs = features[0, 0]
    rows_here, width, chans = inputs.shape
    parts = lax.axis_size("rows")
    full = rows_here * parts
    per_group = chans // GROUPS
    count = full * width * per_group
    extra = time_shift(timestep, time_weight[0], emb_weight[0])
    quarter = conv1_weight.shape[4]
    first = lax.axis_index("rows") * quarter

    def mine(vector):
        return lax.dynamic_slice_in_dim(vector, first, quarter, 0)

    all_rows = gathered_copies(inputs, "rows", 0)
    wide = all_rows.astype(jnp.float32)
    total, square = group_sums(wide, GROUPS)
    act = apply_norm(wide, total, square, count, norm1_gain[0], norm1_shift[0])
    hidden = (convolve(act, conv1_weight[0], "SAME") + mine(conv1_bias[0]) + mine(extra)).astype(
        jnp.bfloat16
    )
    hidden_wide = hidden.astype(jnp.float32)
    total, square = group_sums(hidden_wide, quarter // per_group)
    act_two = apply_norm(
        hidden_wide, total, square, count, mine(norm2_gain[0]), mine(norm2_shift[0])
    )
    piece = gathered_copies(act_two, "rows", 2)
    kernel = lax.slice_in_dim(conv2_weight[0], 0, piece.shape[2], axis=2)
    summed = jnp.zeros((full, width, quarter), jnp.float32) + convolve(piece, kernel, "SAME")
    own_part = lax.dynamic_slice_in_dim(wide, first, quarter, 2)
    partial_block = own_part + summed + mine(conv2_bias[0])
    block = lax.all_to_all(
        as_sent(partial_block), "rows", split_axis=0, concat_axis=2, tiled=True
    ).astype(partial_block.dtype)
    own_out = block.astype(jnp.bfloat16)
    flat = own_out.reshape(-1, chans)
    control = (jnp.dot(flat, zero_weight, preferred_element_type=jnp.float32) + zero_bias).astype(
        jnp.bfloat16
    )
    arrived = from_behind(control.reshape(own_out.shape), "branch", 1)
    result = (block + arrived.astype(jnp.float32)).astype(jnp.bfloat16)
    return result[None, None]


def solution(mesh):
    placed = (
        P("batch"),
        P("batch", "branch", "rows", None, None),
        P("branch", None, None, None, "rows"),
        P("branch", None),
        P("branch", None, None, None, "rows"),
        P("branch", None),
        P("branch", None),
        P("branch", None),
        P("branch", None),
        P("branch", None),
        P("branch", None, None),
        P("branch", None, None),
        P(),
        P(),
    )
    return jax.shard_map(
        body,
        mesh=mesh,
        in_specs=placed,
        out_specs=P("batch", "branch", "rows", None, None),
        check_vma=False,
    )
```

profile of v0, /device:TPU:176, one launch (start us, length us, event | category | flops | bytes accessed | tf_op | source)
XLA Modules:
  0.0 200.0 jit_solution(5692599399322577108)
XLA Ops:
  0.0 1.6 copy.52
  1.6 1.7 broadcast_in_dim.6
  3.3 4.7 %all-to-all-start = ((bf16[4,8,64,640]{3,1,2,0:T(8,128)(2,1)}), bf16[4,8,64,640]{3,1,2,0:T(8,128)(2,1)}, u32[]{:S(2)}, u32[]{:S(2)}) async-start(bf16[4,8,64,640]{3,1,2,0:T(8,128)(2,1)} %broadcast_in_dim.6), calls=%async_computation | async-start | bytes 5242880 | tf_op jit(solution)/shard_map/all_to_all | solution.py:12
  8.0 0.0 copy-done.3
  8.7 0.1 fusion.51
  8.8 0.1 pad_maximum_fusion
  8.8 1.4 convolution_reduce_fusion
  10.3 0.3 fusion.46
  10.6 0.1 dynamic_slice.20
  10.7 0.8 constant_dynamic-slice_fusion.3
  11.5 0.8 constant_dynamic-slice_fusion.1
  12.2 28.1 %all-to-all-done = bf16[4,8,64,640]{3,1,2,0:T(8,128)(2,1)} async-done(((bf16[4,8,64,640]{3,1,2,0:T(8,128)(2,1)}), bf16[4,8,64,640]{3,1,2,0:T(8,128)(2,1)}, u32[]{:S(2)}, u32[]{:S(2)}) %all-to-all-start) | async-done | bytes 2621472 | tf_op jit(solution)/shard_map/all_to_all | solution.py:12
  40.3 2.5 %convert_reduce_fusion = (f32[640]{0:T(1024)S(1)}, f32[640]{0:T(1024)S(1)}) fusion(bf16[4,8,64,640]{3,1,2,0:T(8,128)(2,1)} %all-to-all-done), kind=kLoop, calls=%fused_computation.24 | loop fusion | flops 5241600 | bytes 2626560 | tf_op jit(solution)/shard_map/reduce_sum | solution.py:56
  42.8 0.1 reduce_sum.47
  42.8 0.1 reduce_sum.53
  43.0 0.1 reduce_sum.51
  43.1 0.1 reduce_sum.54
  43.2 0.1 mul.115
  43.3 0.1 mul.116
  43.4 0.1 sub.47
  43.5 0.1 sub.48
  43.6 3.6 %fusion.19 = bf16[32,1,64,640]{3,0,2,1:T(8,128)(2,1)S(1)} fusion(f32[640]{0:T(1024)S(1)} %reduce.9, f32[640]{0:T(1024)S(1)} %reduce.8, f32[640]{0:T(1024)S(1)} %mul.116, f32[640]{0:T(1024)S(1)} %sub.48, bf16[4,8,64,640]{3,1,2,0:T(8,128)(2,1)} %all-to-all-done), kind=kLoop, calls=%fused_computation.25 | loop fusion | flops 13107200 | bytes 5253120 | tf_op jit(solution)/shard_map/convert_element_type | solution.py:66
  47.2 0.2 pad
  47.4 0.0 copy-start.7
  47.4 1.0 copy.56
  48.4 0.2 slice.4
  48.6 9.4 %fusion.20 = (f32[160]{0:T(256)S(1)}, f32[160]{0:T(256)S(1)}, f32[32,8,9,160]{3,1,2,0:T(8,128)}) fusion(pred[8,9]{0,1:T(8,128)(4,1)S(1)} %copy-done.7, f32[160]{0:T(256)S(1)} %dynamic_slice.20, f32[160]{0:T(256)S(1)} %bitcast.96, bf16[1,3,3,640,160]{3,4,2,1,0:T(8,128)(2,1)S(1)} %copy-done, bf16[32,1,7,2,640]{4,2,3,0,1:T(8,128)(2,1)S(1)} %slice.4, ...), kind=kOutput, calls=%fused_computation.26 | convolution fusion | flops 4172758528 | bytes 6842952 | tf_op jit(solution)/shard_map/conv_general_dilated | solution.py:70
  58.0 0.1 reduce_sum.59
  58.1 0.1 reduce_sum.72
  58.2 0.1 reduce_sum.74
  58.3 0.1 reduce_sum.75
  58.5 0.1 mul.128
  58.5 0.1 mul.129
  58.6 0.1 sub.52
  58.7 0.1 sub.53
  58.8 2.4 %copy.57 = f32[32,8,9,160]{3,0,2,1:T(8,128)S(1)} copy(f32[32,8,9,160]{3,1,2,0:T(8,128)} %get-tuple-element.13) | data formatting | bytes 2949120 | tf_op jit(solution)/shard_map/conv_general_dilated | solution.py:70
  61.2 0.8 multiply_convert_fusion.1
  62.0 0.6 copy.58
  62.6 14.3 %broadcast_in_dim.7 = bf16[4,32,64,160]{3,2,1,0:T(8,128)(2,1)} broadcast(bf16[32,64,160]{2,1,0:T(8,128)(2,1)S(1)} %copy.58), dimensions={1,2,3} | broadcast | bytes 3276800 | tf_op jit(solution)/shard_map/broadcast_in_dim | solution.py:11
  76.9 4.9 %all-to-all-start.1 = ((bf16[4,32,64,160]{3,2,1,0:T(8,128)(2,1)}), bf16[4,32,64,160]{3,2,1,0:T(8,128)(2,1)}, u32[]{:S(2)}, u32[]{:S(2)}) async-start(bf16[4,32,64,160]{3,2,1,0:T(8,128)(2,1)} %broadcast_in_dim.7), calls=%async_computation.1 | async-start | bytes 8388608 | tf_op jit(solution)/shard_map/all_to_all | solution.py:12
  81.8 0.8 constant_dynamic-slice_fusion
  82.6 4.7 %copy_bitcast_fusion = f32[32,64,640]{2,0,1:T(8,128)} fusion(bf16[4,8,64,640]{3,1,2,0:T(8,128)(2,1)} %all-to-all-done), kind=kLoop, calls=%fused_computation.9 | loop fusion | flops 1310720 | bytes 7864320 | tf_op jit(solution)/shard_map/convert_element_type | solution.py:110
  87.3 42.8 %all-to-all-done.1 = bf16[4,32,64,160]{3,2,1,0:T(8,128)(2,1)} async-done(((bf16[4,32,64,160]{3,2,1,0:T(8,128)(2,1)}), bf16[4,32,64,160]{3,2,1,0:T(8,128)(2,1)}, u32[]{:S(2)}, u32[]{:S(2)}) %all-to-all-start.1) | async-done | bytes 2621472 | tf_op jit(solution)/shard_map/all_to_all | solution.py:12
  130.1 7.5 %copy.68 = bf16[32,64,4,160]{3,2,0,1:T(4,128)(2,1)} copy(bf16[32,64,4,160]{3,1,0,2:T(8,128)(2,1)} %bitcast.15) | data formatting | bytes 5242880
  137.6 7.9 %reshape.170 = bf16[32,1,64,640]{3,0,2,1:T(8,128)(2,1)} reshape(bf16[32,64,4,160]{3,2,0,1:T(4,128)(2,1)} %copy.68) | data formatting | bytes 5242880
  145.5 2.0 pad.2.clone
  147.4 0.0 copy-start.5
  147.5 1.0 copy.62
  148.5 0.2 slice.6
  148.6 0.3 copy-done.5
  148.9 8.4 %fusion.35 = f32[32,8,9,160]{3,1,2,0:T(8,128)S(1)} fusion(bf16[1,3,3,640,160]{3,4,2,1,0:T(8,128)(2,1)S(1)} %copy-done.5, bf16[32,1,7,2,640]{4,2,3,0,1:T(8,128)(2,1)S(1)} %slice.6, bf16[32,1,8,9,640]{4,2,3,0,1:T(8,128)(2,1)S(1)} %copy.62, pred[8,9]{0,1:T(8,128)(4,1)S(1)} %copy-done.7), kind=kOutput, calls=%fused_computation.45 | convolution fusion | flops 4169441280 | bytes 6840392 | tf_op jit(solution)/shard_map/conv_general_dilated | solution.py:70
  157.3 0.8 copy.63
  158.1 2.6 %fusion.25 = bf16[32,64,160]{2,0,1:T(8,128)(2,1)S(1)} fusion(f32[32,1,72,160]{3,0,2,1:T(8,128)S(1)} %bitcast.94, f32[32,64,640]{2,0,1:T(8,128)} %copy_bitcast_fusion, s32[]{:T(128)S(6)} %select_n.2, f32[160]{0:T(256)S(1)} %bitcast.98), kind=kLoop, calls=%fused_computation.33 | loop fusion | flops 983040 | bytes 3277444 | tf_op jit(solution)/shard_map/convert_element_type | solution.py:29
  160.7 0.6 copy.64
  161.3 16.1 %all_to_all.25 = bf16[32,64,160]{2,1,0:T(8,128)(2,1)S(1)} all-to-all(bf16[32,64,160]{2,1,0:T(8,128)(2,1)S(1)} %copy.64), channel_id=1, replica_groups=mesh['branch'=2,'batch'=32,'rows'=4] {'rows'}, dimensions={0} | all-to-all | bytes 1310720 | tf_op jit(solution)/shard_map/all_to_all | solution.py:126
  177.4 0.8 copy.66
  178.2 0.6 reshape.128
  178.9 2.7 %fusion.45 = bf16[512,640]{1,0:T(8,128)(2,1)} fusion(bf16[512,640]{1,0:T(8,128)(2,1)S(1)} %reshape.128, bf16[640,640]{1,0:T(8,128)(2,1)} %param.26, f32[640]{0:T(1024)S(1)} %copy-done.6), kind=kOutput, calls=%fused_computation.48 | convolution fusion | flops 420085760 | bytes 2132480 | tf_op jit(solution)/shard_map/dot_general | solution.py:131
  181.6 1.3 collective-permute-start
  182.9 0.0 copy-start.1
  182.9 2.2 %copy.65 = f32[8,64,4,160]{3,2,1,0:T(4,128)} copy(bf16[8,64,4,160]{3,1,0,2:T(8,128)(2,1)S(1)} %bitcast.92) | data formatting | bytes 1966080 | tf_op jit(solution)/shard_map/convert_element_type | solution.py:128
  185.1 2.6 %reshape.148 = f32[8,64,640]{2,1,0:T(8,128)S(1)} reshape(f32[8,64,4,160]{3,2,1,0:T(4,128)} %copy.65) | data formatting | bytes 2621440 | tf_op jit(solution)/shard_map/convert_element_type | solution.py:128
  187.7 10.0 %collective-permute-done = bf16[8,64,640]{2,1,0:T(8,128)(2,1)} collective-permute-done((bf16[8,64,640]{2,1,0:T(8,128)(2,1)}, bf16[8,64,640]{2,1,0:T(8,128)(2,1)}, u32[]{:S(2)}, u32[]{:S(2)}) %collective-permute-start) | collective-permute-done | bytes 655392 | tf_op jit(solution)/shard_map/ppermute | solution.py:37
  197.7 2.1 %fusion.50 = bf16[1,1,8,64,640]{4,3,2,1,0:T(8,128)(2,1)} fusion(f32[8,64,640]{2,1,0:T(8,128)S(1)} %reshape.148, bf16[8,64,640]{2,1,0:T(8,128)(2,1)} %collective-permute-done), kind=kLoop, calls=%fused_computation.53 | loop fusion | flops 983040 | bytes 2621440 | tf_op jit(solution)/shard_map/broadcast_in_dim | solution.py:136
  (18 shorter events, 0.1 us)
Async XLA Ops:
  0.0 48.6 %copy-start = (bf16[1,3,3,640,160]{3,4,2,1,0:T(8,128)(2,1)S(1)}, bf16[1,3,3,640,160]{3,4,2,1,0:T(8,128)(2,1)}, u32[]{:S(2)}) copy-start(bf16[1,3,3,640,160]{3,4,2,1,0:T(8,128)(2,1)} %param.16) | copy-start | bytes 5529604
  3.3 4.7 %copy-start.3 = (f32[1,640]{1,0:T(1,128)S(1)}, f32[1,640]{1,0:T(1,128)}, u32[]{:S(2)}) copy-start(f32[1,640]{1,0:T(1,128)} %param.20) | copy-start | bytes 7684
  3.3 4.7 %copy-start.4 = (f32[1,640]{1,0:T(1,128)S(1)}, f32[1,640]{1,0:T(1,128)}, u32[]{:S(2)}) copy-start(f32[1,640]{1,0:T(1,128)} %param.21) | copy-start | bytes 7684
  3.3 7.0 %copy-start.2 = (bf16[1,1280,640]{2,1,0:T(8,128)(2,1)S(1)}, bf16[1,1280,640]{2,1,0:T(8,128)(2,1)}, u32[]{:S(2)}) copy-start(bf16[1,1280,640]{2,1,0:T(8,128)(2,1)} %param.25) | copy-start | bytes 4915204
  3.3 37.0 %all-to-all-start = ((bf16[4,8,64,640]{3,1,2,0:T(8,128)(2,1)}), bf16[4,8,64,640]{3,1,2,0:T(8,128)(2,1)}, u32[]{:S(2)}, u32[]{:S(2)}) async-start(bf16[4,8,64,640]{3,1,2,0:T(8,128)(2,1)} %broadcast_in_dim.6), calls=%async_computation | async-start | bytes 5242880 | tf_op jit(solution)/shard_map/all_to_all | solution.py:12
  47.4 1.2 copy-start.7
  76.9 53.2 %all-to-all-start.1 = ((bf16[4,32,64,160]{3,2,1,0:T(8,128)(2,1)}), bf16[4,32,64,160]{3,2,1,0:T(8,128)(2,1)}, u32[]{:S(2)}, u32[]{:S(2)}) async-start(bf16[4,32,64,160]{3,2,1,0:T(8,128)(2,1)} %broadcast_in_dim.7), calls=%async_computation.1 | async-start | bytes 8388608 | tf_op jit(solution)/shard_map/all_to_all | solution.py:12
  147.4 1.5 copy-start.5
  177.4 1.5 copy-start.6
  181.6 16.1 %collective-permute-start = (bf16[8,64,640]{2,1,0:T(8,128)(2,1)}, bf16[8,64,640]{2,1,0:T(8,128)(2,1)}, u32[]{:S(2)}, u32[]{:S(2)}) collective-permute-start(bf16[8,64,640]{2,1,0:T(8,128)(2,1)} %bitcast.25), channel_id=1, source_target_pairs={{0,128},{1,129},{2,130},{3,131},{4,132},{5,133},{6,134},{7,135},{8... | collective-permute-start | bytes 1966088 | tf_op jit(solution)/shard_map/ppermute | solution.py:37
  182.9 16.9 %copy-start.1 = (bf16[1,3,3,640,160]{3,4,2,1,0:T(8,128)(2,1)S(1)}, bf16[1,3,3,640,160]{3,4,2,1,0:T(8,128)(2,1)}, u32[]{:S(2)}) copy-start(bf16[1,3,3,640,160]{3,4,2,1,0:T(8,128)(2,1)} %param.16) | copy-start | bytes 5529604
where the time goes:
time: 204 us; the launch traced here: 200 us
  waiting for transfers between devices  80.9 us (40%)
  local copies, waits for them, and re-layouts  51.9 us (25%)
  matrix products  22.2 us (11%)
  other arithmetic  16.9 us (8%)
  blocking collectives  16.1 us (8%)
  starting transfers between devices  10.8 us (5%)
    all_to_all x2, waiting for transfers between devices, from_everyone(): return lax.all_to_all(copies, axis, split_axis=0, concat_axis=0, tiled=True)  70.9 us
    conv_general_dilated x2, matrix products, convolve(): lax.conv_general_dilated(inputs[None], kernel, (1, 1), padding, dimension...  17.8 us
    all_to_all x1, blocking collectives, body(): lax.all_to_all(as_sent(partial_block), 'rows', split_axis=0, concat_axis=...  16.1 us
    broadcast_in_dim x2, local copies, waits for them, and re-layouts, from_everyone(): copies = jnp.broadcast_to(x, (lax.axis_size(axis), *x.shape))  16 us
    unnamed x18, local copies, waits for them, and re-layouts  15.7 us
    ppermute x1, waiting for transfers between devices, from_behind(): return lax.ppermute(x, axis, pairs)  10 us
    all_to_all x2, starting transfers between devices, from_everyone(): return lax.all_to_all(copies, axis, split_axis=0, concat_axis=0, tiled=True)  9.55 us
    conv_general_dilated x6, local copies, waits for them, and re-layouts, convolve(): lax.conv_general_dilated(inputs[None], kernel, (1, 1), padding, dimension...  5.51 us
  transfers between devices with their start and end apart: 3, of which 3 were waited for; matrix products, arithmetic and copies ran while one was open for 7% of the time, Pallas kernels for 0%

commit v1 on v0

--- a/solution.py
+++ b/solution.py
@@ -5,6 +5,37 @@
 from jax.sharding import PartitionSpec as P
 
 GROUPS = 32
+
+
+def start_the_squares(my_tile, along_dim, arr_in):
+    x_new, later = (my_tile.shape[:along_dim], my_tile.shape[along_dim + 1 :])
+    v1 = jnp.moveaxis(my_tile.reshape(*x_new, arr_in, -1, *later), along_dim, 0)
+    return v1
+
+
+def search_kinds(patch, array_axis):
+    patch = jnp.moveaxis(patch, 0, array_axis)
+    spare = patch.shape
+    plain = patch.reshape(
+        *spare[:array_axis], spare[array_axis] * spare[array_axis + 1], *spare[array_axis + 2 :]
+    )
+    return plain
+
+
+def replace_column(payload, across, local_x, mat=2):
+    arr_next, ready = (jax.lax.psum(1, axis_name=across), jax.lax.axis_index(across))
+    v_next = start_the_squares(payload, local_x, arr_next)
+    leaves = [v_next[ready]]
+    m = 1
+    while m < arr_next:
+        upper = v_next[ready ^ m]
+        leaves.append(
+            jax.lax.ppermute(upper, axis_name=across, perm=[(w, w ^ m) for w in range(arr_next)])
+        )
+        m += 1
+    v_next = jnp.stack(leaves, axis=0)[ready ^ jnp.arange(arr_next)]
+    outer = search_kinds(v_next, mat)
+    return outer
 
 
 def from_everyone(x, axis):
@@ -123,9 +154,7 @@
     summed = jnp.zeros((full, width, quarter), jnp.float32) + convolve(piece, kernel, "SAME")
     own_part = lax.dynamic_slice_in_dim(wide, first, quarter, 2)
     partial_block = own_part + summed + mine(conv2_bias[0])
-    block = lax.all_to_all(
-        as_sent(partial_block), "rows", split_axis=0, concat_axis=2, tiled=True
-    ).astype(partial_block.dtype)
+    block = replace_column(as_sent(partial_block), "rows", 0).astype(partial_block.dtype)
     own_out = block.astype(jnp.bfloat16)
     flat = own_out.reshape(-1, chans)
     control = (jnp.dot(flat, zero_weight, preferred_element_type=jnp.float32) + zero_bias).astype(

time: 204 us -> 205 us (level)
  blocking collectives: 16.1 us -> 0 us
  waiting for transfers between devices: 80.9 us -> 91.4 us
  starting transfers between devices: 10.8 us -> 15.6 us
    all_to_all x1 -> x0, blocking collectives: 16.1 us -> none  [body(): lax.all_to_all(as_sent(partial_block), 'rows', split_axis=0, concat_axis=...]
    ppermute x0 -> x3, waiting for transfers between devices: none -> 10.2 us  [replace_column(): jax.lax.ppermute(upper, axis_name=across, perm=[(w, w ^ m) for w in range...]
    ppermute x0 -> x3, starting transfers between devices: none -> 4.79 us  [replace_column(): jax.lax.ppermute(upper, axis_name=across, perm=[(w, w ^ m) for w in range...]
  transfers between devices with their start and end apart: 3 -> 6, of which waited for: 3 -> 6; matrix products, arithmetic and copies ran while one was open for 7% -> 7% of each run, Pallas kernels for 0% -> 0%
where the time goes in v1:
time: 205 us; the launch traced here: 202 us
  waiting for transfers between devices  91.4 us (45%)
  local copies, waits for them, and re-layouts  53.6 us (26%)
  matrix products  22.3 us (11%)
  other arithmetic  17.4 us (8%)
  starting transfers between devices  15.6 us (8%)
    all_to_all x2, waiting for transfers between devices, from_everyone(): return lax.all_to_all(copies, axis, split_axis=0, concat_axis=0, tiled=True)  70.8 us
    conv_general_dilated x2, matrix products, convolve(): lax.conv_general_dilated(inputs[None], kernel, (1, 1), padding, dimension...  17.8 us
    broadcast_in_dim x2, local copies, waits for them, and re-layouts, from_everyone(): copies = jnp.broadcast_to(x, (lax.axis_size(axis), *x.shape))  16.5 us
    unnamed x18, local copies, waits for them, and re-layouts  15.7 us
    ppermute x1, waiting for transfers between devices, from_behind(): return lax.ppermute(x, axis, pairs)  10.3 us
    ppermute x3, waiting for transfers between devices, replace_column(): jax.lax.ppermute(upper, axis_name=across, perm=[(w, w ^ m) for w in range...  10.2 us
    all_to_all x2, starting transfers between devices, from_everyone(): return lax.all_to_all(copies, axis, split_axis=0, concat_axis=0, tiled=True)  9.55 us
    conv_general_dilated x6, local copies, waits for them, and re-layouts, convolve(): lax.conv_general_dilated(inputs[None], kernel, (1, 1), padding, dimension...  5.51 us
  transfers between devices with their start and end apart: 6, of which 6 were waited for; matrix products, arithmetic and copies ran while one was open for 7% of the time, Pallas kernels for 0%

profile of v1, /device:TPU:176, one launch (start us, length us, event | category | flops | bytes accessed | tf_op | source)
XLA Modules:
  0.0 201.5 jit_solution(13864157463818140079)
XLA Ops:
  0.0 1.6 copy.52
  1.6 1.7 broadcast_in_dim.6
  3.3 4.7 %all-to-all-start = ((bf16[4,8,64,640]{3,1,2,0:T(8,128)(2,1)}), bf16[4,8,64,640]{3,1,2,0:T(8,128)(2,1)}, u32[]{:S(2)}, u32[]{:S(2)}) async-start(bf16[4,8,64,640]{3,1,2,0:T(8,128)(2,1)} %broadcast_in_dim.6), calls=%async_computation | async-start | bytes 5242880 | tf_op jit(solution)/shard_map/all_to_all | solution.py:43
  8.7 0.1 pad_maximum_fusion.1
  8.8 1.4 convolution_reduce_fusion
  10.3 0.3 fusion.46
  10.6 0.1 dynamic_slice.32
  10.7 0.8 constant_dynamic-slice_fusion.4
  11.4 0.8 constant_dynamic-slice_fusion.2
  12.2 28.1 %all-to-all-done = bf16[4,8,64,640]{3,1,2,0:T(8,128)(2,1)} async-done(((bf16[4,8,64,640]{3,1,2,0:T(8,128)(2,1)}), bf16[4,8,64,640]{3,1,2,0:T(8,128)(2,1)}, u32[]{:S(2)}, u32[]{:S(2)}) %all-to-all-start) | async-done | bytes 2621472 | tf_op jit(solution)/shard_map/all_to_all | solution.py:43
  40.3 2.5 %convert_reduce_fusion = (f32[640]{0:T(1024)S(1)}, f32[640]{0:T(1024)S(1)}) fusion(bf16[4,8,64,640]{3,1,2,0:T(8,128)(2,1)} %all-to-all-done), kind=kLoop, calls=%fused_computation.25 | loop fusion | flops 5241600 | bytes 2626560 | tf_op jit(solution)/shard_map/reduce_sum | solution.py:87
  42.8 0.1 reduce_sum.47
  42.8 0.1 reduce_sum.53
  43.0 0.1 reduce_sum.51
  43.1 0.1 reduce_sum.54
  43.3 0.1 mul.116
  43.5 0.1 sub.48
  43.6 3.6 %fusion.19 = bf16[32,1,64,640]{3,0,2,1:T(8,128)(2,1)S(1)} fusion(f32[640]{0:T(1024)S(1)} %reduce.9, f32[640]{0:T(1024)S(1)} %reduce.8, f32[640]{0:T(1024)S(1)} %mul.116, f32[640]{0:T(1024)S(1)} %sub.48, bf16[4,8,64,640]{3,1,2,0:T(8,128)(2,1)} %all-to-all-done), kind=kLoop, calls=%fused_computation.26 | loop fusion | flops 13107200 | bytes 5253120 | tf_op jit(solution)/shard_map/convert_element_type | solution.py:97
  47.2 0.2 pad
  47.4 1.0 copy.56
  48.4 0.2 slice.6
  48.6 9.4 %fusion.20 = (f32[160]{0:T(256)S(1)}, f32[160]{0:T(256)S(1)}, f32[32,8,9,160]{3,1,2,0:T(8,128)}) fusion(pred[8,9]{0,1:T(8,128)(4,1)S(1)} %copy-done.7, f32[160]{0:T(256)S(1)} %dynamic_slice.32, f32[160]{0:T(256)S(1)} %bitcast.110, bf16[1,3,3,640,160]{3,4,2,1,0:T(8,128)(2,1)S(1)} %copy-done, bf16[32,1,7,2,640]{4,2,3,0,1:T(8,128)(2,1)S(1)} %slice.6, ...), kind=kOutput, calls=%fused_computation.27 | convolution fusion | flops 4172758528 | bytes 6842952 | tf_op jit(solution)/shard_map/conv_general_dilated | solution.py:101
  58.0 0.1 reduce_sum.59
  58.1 0.1 reduce_sum.72
  58.2 0.1 reduce_sum.74
  58.3 0.1 reduce_sum.75
  58.5 0.1 mul.129
  58.7 0.1 sub.53
  58.8 2.4 %copy.57 = f32[32,8,9,160]{3,0,2,1:T(8,128)S(1)} copy(f32[32,8,9,160]{3,1,2,0:T(8,128)} %get-tuple-element.17) | data formatting | bytes 2949120 | tf_op jit(solution)/shard_map/conv_general_dilated | solution.py:101
  61.2 0.8 multiply_convert_fusion.1
  62.0 0.6 copy.58
  62.6 14.8 %broadcast_in_dim.7 = bf16[4,32,64,160]{3,2,1,0:T(8,128)(2,1)} broadcast(bf16[32,64,160]{2,1,0:T(8,128)(2,1)S(1)} %copy.58), dimensions={1,2,3} | broadcast | bytes 3276800 | tf_op jit(solution)/shard_map/broadcast_in_dim | solution.py:42
  77.4 4.9 %all-to-all-start.1 = ((bf16[4,32,64,160]{3,2,1,0:T(8,128)(2,1)}), bf16[4,32,64,160]{3,2,1,0:T(8,128)(2,1)}, u32[]{:S(2)}, u32[]{:S(2)}) async-start(bf16[4,32,64,160]{3,2,1,0:T(8,128)(2,1)} %broadcast_in_dim.7), calls=%async_computation.1 | async-start | bytes 8388608 | tf_op jit(solution)/shard_map/all_to_all | solution.py:43
  82.3 0.8 constant_dynamic-slice_fusion.1
  83.1 4.7 %copy_bitcast_fusion = f32[32,64,640]{2,0,1:T(8,128)} fusion(bf16[4,8,64,640]{3,1,2,0:T(8,128)(2,1)} %all-to-all-done), kind=kLoop, calls=%fused_computation.10 | loop fusion | flops 1310720 | bytes 7864320 | tf_op jit(solution)/shard_map/convert_element_type | solution.py:141
  87.8 42.8 %all-to-all-done.1 = bf16[4,32,64,160]{3,2,1,0:T(8,128)(2,1)} async-done(((bf16[4,32,64,160]{3,2,1,0:T(8,128)(2,1)}), bf16[4,32,64,160]{3,2,1,0:T(8,128)(2,1)}, u32[]{:S(2)}, u32[]{:S(2)}) %all-to-all-start.1) | async-done | bytes 2621472 | tf_op jit(solution)/shard_map/all_to_all | solution.py:43
  130.6 7.5 %copy.68 = bf16[32,64,4,160]{3,2,0,1:T(4,128)(2,1)} copy(bf16[32,64,4,160]{3,1,0,2:T(8,128)(2,1)} %bitcast.15) | data formatting | bytes 5242880
  138.1 7.9 %reshape.199 = bf16[32,1,64,640]{3,0,2,1:T(8,128)(2,1)} reshape(bf16[32,64,4,160]{3,2,0,1:T(4,128)(2,1)} %copy.68) | data formatting | bytes 5242880
  146.0 2.0 pad.2.clone
  148.0 1.0 copy.62
  149.0 0.2 slice.8
  149.1 0.3 copy-done.5
  149.4 8.4 %fusion.35 = f32[32,8,9,160]{3,1,2,0:T(8,128)S(1)} fusion(bf16[1,3,3,640,160]{3,4,2,1,0:T(8,128)(2,1)S(1)} %copy-done.5, bf16[32,1,7,2,640]{4,2,3,0,1:T(8,128)(2,1)S(1)} %slice.8, bf16[32,1,8,9,640]{4,2,3,0,1:T(8,128)(2,1)S(1)} %copy.62, pred[8,9]{0,1:T(8,128)(4,1)S(1)} %copy-done.7), kind=kOutput, calls=%fused_computation.46 | convolution fusion | flops 4169441280 | bytes 6840392 | tf_op jit(solution)/shard_map/conv_general_dilated | solution.py:101
  157.8 0.8 copy.63
  158.6 2.6 %fusion.25 = bf16[32,64,160]{2,0,1:T(8,128)(2,1)S(1)} fusion(f32[32,1,72,160]{3,0,2,1:T(8,128)S(1)} %bitcast.104, f32[32,64,640]{2,0,1:T(8,128)} %copy_bitcast_fusion, s32[]{:T(128)S(6)} %select_n.30, f32[160]{0:T(256)S(1)} %bitcast.112), kind=kLoop, calls=%fused_computation.34 | loop fusion | flops 983040 | bytes 3277444 | tf_op jit(solution)/shard_map/convert_element_type | solution.py:60
  161.2 0.6 copy.64
  161.8 0.1 constant_dynamic-slice_fusion
  161.9 0.6 collective-permute-start
  162.6 1.8 collective-permute-start.1
  164.3 2.4 %collective-permute-start.2 = (bf16[8,64,160]{2,1,0:T(8,128)(2,1)S(1)}, bf16[8,64,160]{2,1,0:T(8,128)(2,1)S(1)}, u32[]{:S(2)}, u32[]{:S(2)}) collective-permute-start(bf16[8,64,160]{2,1,0:T(8,128)(2,1)S(1)} %get-tuple-element.10), channel_id=1, source_target_pairs={{0,3},{1,2},{2,1},{3,0},{4,7},{5,6},{6,5},{7,4},{8,11},{9,10},{10,... | collective-permute-start | bytes 491528 | tf_op jit(solution)/shard_map/ppermute | solution.py:33
  166.7 4.4 %collective-permute-done = bf16[8,64,160]{2,1,0:T(8,128)(2,1)S(1)} collective-permute-done((bf16[8,64,160]{2,1,0:T(8,128)(2,1)S(1)}, bf16[8,64,160]{2,1,0:T(8,128)(2,1)S(1)}, u32[]{:S(2)}, u32[]{:S(2)}) %collective-permute-start) | collective-permute-done | bytes 163872 | tf_op jit(solution)/shard_map/ppermute | solution.py:33
  171.1 3.1 %collective-permute-done.1 = bf16[8,64,160]{2,1,0:T(8,128)(2,1)S(1)} collective-permute-done((bf16[8,64,160]{2,1,0:T(8,128)(2,1)S(1)}, bf16[8,64,160]{2,1,0:T(8,128)(2,1)S(1)}, u32[]{:S(2)}, u32[]{:S(2)}) %collective-permute-start.1) | collective-permute-done | bytes 163872 | tf_op jit(solution)/shard_map/ppermute | solution.py:33
  174.2 2.7 %collective-permute-done.2 = bf16[8,64,160]{2,1,0:T(8,128)(2,1)S(1)} collective-permute-done((bf16[8,64,160]{2,1,0:T(8,128)(2,1)S(1)}, bf16[8,64,160]{2,1,0:T(8,128)(2,1)S(1)}, u32[]{:S(2)}, u32[]{:S(2)}) %collective-permute-start.2) | collective-permute-done | bytes 163872 | tf_op jit(solution)/shard_map/ppermute | solution.py:33
  176.9 0.2 pad_maximum_fusion
  177.2 0.6 gather_fusion
  177.8 0.8 copy.66
  178.6 0.7 reshape.149
  179.3 2.7 %fusion.45 = bf16[512,640]{1,0:T(8,128)(2,1)} fusion(bf16[512,640]{1,0:T(8,128)(2,1)S(1)} %reshape.149, bf16[640,640]{1,0:T(8,128)(2,1)} %param.26, f32[640]{0:T(1024)S(1)} %copy-done.6), kind=kOutput, calls=%fused_computation.49 | convolution fusion | flops 420085760 | bytes 2132480 | tf_op jit(solution)/shard_map/dot_general | solution.py:160
  182.0 1.3 collective-permute-start.3
  183.3 0.2 bitcast_convert_fusion
  183.6 2.7 %copy.65 = f32[8,64,4,160]{3,2,1,0:T(4,128)} copy(f32[8,64,4,160]{3,1,0,2:T(8,128)S(1)} %bitcast_convert_fusion) | data formatting | bytes 2621440 | tf_op jit(solution)/shard_map/convert_element_type | solution.py:157
  186.3 2.6 %reshape.169 = f32[8,64,640]{2,1,0:T(8,128)S(1)} reshape(f32[8,64,4,160]{3,2,1,0:T(4,128)} %copy.65) | data formatting | bytes 2621440 | tf_op jit(solution)/shard_map/convert_element_type | solution.py:157
  188.9 10.3 %collective-permute-done.3 = bf16[8,64,640]{2,1,0:T(8,128)(2,1)} collective-permute-done((bf16[8,64,640]{2,1,0:T(8,128)(2,1)}, bf16[8,64,640]{2,1,0:T(8,128)(2,1)}, u32[]{:S(2)}, u32[]{:S(2)}) %collective-permute-start.3) | collective-permute-done | bytes 655392 | tf_op jit(solution)/shard_map/ppermute | solution.py:68
  199.2 2.1 %fusion.50 = bf16[1,1,8,64,640]{4,3,2,1,0:T(8,128)(2,1)} fusion(f32[8,64,640]{2,1,0:T(8,128)S(1)} %reshape.169, bf16[8,64,640]{2,1,0:T(8,128)(2,1)} %collective-permute-done.3), kind=kLoop, calls=%fused_computation.55 | loop fusion | flops 983040 | bytes 2621440 | tf_op jit(solution)/shard_map/broadcast_in_dim | solution.py:165
  (29 shorter events, 0.5 us)
Async XLA Ops:
  0.0 48.6 %copy-start = (bf16[1,3,3,640,160]{3,4,2,1,0:T(8,128)(2,1)S(1)}, bf16[1,3,3,640,160]{3,4,2,1,0:T(8,128)(2,1)}, u32[]{:S(2)}) copy-start(bf16[1,3,3,640,160]{3,4,2,1,0:T(8,128)(2,1)} %param.16) | copy-start | bytes 5529604
  3.3 6.9 %copy-start.3 = (f32[1,640]{1,0:T(1,128)S(1)}, f32[1,640]{1,0:T(1,128)}, u32[]{:S(2)}) copy-start(f32[1,640]{1,0:T(1,128)} %param.20) | copy-start | bytes 7684
  3.3 6.9 %copy-start.4 = (f32[1,640]{1,0:T(1,128)S(1)}, f32[1,640]{1,0:T(1,128)}, u32[]{:S(2)}) copy-start(f32[1,640]{1,0:T(1,128)} %param.21) | copy-start | bytes 7684
  3.3 7.0 %copy-start.2 = (bf16[1,1280,640]{2,1,0:T(8,128)(2,1)S(1)}, bf16[1,1280,640]{2,1,0:T(8,128)(2,1)}, u32[]{:S(2)}) copy-start(bf16[1,1280,640]{2,1,0:T(8,128)(2,1)} %param.25) | copy-start | bytes 4915204
  3.3 37.0 %all-to-all-start = ((bf16[4,8,64,640]{3,1,2,0:T(8,128)(2,1)}), bf16[4,8,64,640]{3,1,2,0:T(8,128)(2,1)}, u32[]{:S(2)}, u32[]{:S(2)}) async-start(bf16[4,8,64,640]{3,1,2,0:T(8,128)(2,1)} %broadcast_in_dim.6), calls=%async_computation | async-start | bytes 5242880 | tf_op jit(solution)/shard_map/all_to_all | solution.py:43
  47.4 1.2 copy-start.7
  77.4 53.2 %all-to-all-start.1 = ((bf16[4,32,64,160]{3,2,1,0:T(8,128)(2,1)}), bf16[4,32,64,160]{3,2,1,0:T(8,128)(2,1)}, u32[]{:S(2)}, u32[]{:S(2)}) async-start(bf16[4,32,64,160]{3,2,1,0:T(8,128)(2,1)} %broadcast_in_dim.7), calls=%async_computation.1 | async-start | bytes 8388608 | tf_op jit(solution)/shard_map/all_to_all | solution.py:43
  147.9 1.5 copy-start.5
  161.9 9.2 %collective-permute-start = (bf16[8,64,160]{2,1,0:T(8,128)(2,1)S(1)}, bf16[8,64,160]{2,1,0:T(8,128)(2,1)S(1)}, u32[]{:S(2)}, u32[]{:S(2)}) collective-permute-start(bf16[8,64,160]{2,1,0:T(8,128)(2,1)S(1)} %get-tuple-element.12), channel_id=1, source_target_pairs={{0,1},{1,0},{2,3},{3,2},{4,5},{5,4},{6,7},{7,6},{8,9},{9,8},{10,11... | collective-permute-start | bytes 491528 | tf_op jit(solution)/shard_map/ppermute | solution.py:33
  162.6 11.7 %collective-permute-start.1 = (bf16[8,64,160]{2,1,0:T(8,128)(2,1)S(1)}, bf16[8,64,160]{2,1,0:T(8,128)(2,1)S(1)}, u32[]{:S(2)}, u32[]{:S(2)}) collective-permute-start(bf16[8,64,160]{2,1,0:T(8,128)(2,1)S(1)} %get-tuple-element.11), channel_id=1, source_target_pairs={{0,2},{1,3},{2,0},{3,1},{4,6},{5,7},{6,4},{7,5},{8,10},{9,11},{10,... | collective-permute-start | bytes 491528 | tf_op jit(solution)/shard_map/ppermute | solution.py:33
  164.3 12.6 %collective-permute-start.2 = (bf16[8,64,160]{2,1,0:T(8,128)(2,1)S(1)}, bf16[8,64,160]{2,1,0:T(8,128)(2,1)S(1)}, u32[]{:S(2)}, u32[]{:S(2)}) collective-permute-start(bf16[8,64,160]{2,1,0:T(8,128)(2,1)S(1)} %get-tuple-element.10), channel_id=1, source_target_pairs={{0,3},{1,2},{2,1},{3,0},{4,7},{5,6},{6,5},{7,4},{8,11},{9,10},{10,... | collective-permute-start | bytes 491528 | tf_op jit(solution)/shard_map/ppermute | solution.py:33
  177.8 1.5 copy-start.6
  182.0 17.2 %collective-permute-start.3 = (bf16[8,64,640]{2,1,0:T(8,128)(2,1)}, bf16[8,64,640]{2,1,0:T(8,128)(2,1)}, u32[]{:S(2)}, u32[]{:S(2)}) collective-permute-start(bf16[8,64,640]{2,1,0:T(8,128)(2,1)} %bitcast.31), channel_id=1, source_target_pairs={{0,128},{1,129},{2,130},{3,131},{4,132},{5,133},{6,134},{7,135},{8... | collective-permute-start | bytes 1966088 | tf_op jit(solution)/shard_map/ppermute | solution.py:68
  183.6 17.8 %copy-start.1 = (bf16[1,3,3,640,160]{3,4,2,1,0:T(8,128)(2,1)S(1)}, bf16[1,3,3,640,160]{3,4,2,1,0:T(8,128)(2,1)}, u32[]{:S(2)}) copy-start(bf16[1,3,3,640,160]{3,4,2,1,0:T(8,128)(2,1)} %param.16) | copy-start | bytes 5529604
